TPU v7x, 32 devices: a whole 2x2x4 slice. The times are simulated.
32 devices in a mesh: section: 4 (over x, core), tensor: 8 (over z, y).
Axes of the slice: x: 2, y: 2, z: 4, core: 2. Of those that a mesh axis runs over, the one named last changes fastest.
Arguments:
- hidden_in: bfloat16 [64, 2560], P(None, 'tensor'), may hold values from -6 to 6
- pre_gain: float32 [4, 2560], P('section'), may hold values from 0.1 to 1.9
- w_zx: bfloat16 [4, 2560, 80, 128], P('section', None, 'tensor'), may hold values from -0.125 to 0.125
- w_bc: bfloat16 [4, 2560, 256], P('section'), may hold values from -0.125 to 0.125
- w_dt: bfloat16 [4, 2560, 80], P('section', None, 'tensor'), may hold values from -0.125 to 0.125
- dt_bias: float32 [4, 80], P('section', 'tensor'), may hold values from -4 to -1
- a_log: float32 [4, 80], P('section', 'tensor'), may hold values from 0 to 2.77
- d_skip: float32 [4, 80], P('section', 'tensor'), may hold values from 0.5 to 2
- conv_x_weight: float32 [4, 4, 80, 64], P('section', None, 'tensor'), may hold values from -3 to 3
- conv_x_bias: float32 [4, 80, 64], P('section', 'tensor'), may hold values from -3 to 3
- conv_bc_weight: float32 [4, 4, 256], P('section'), may hold values from -3 to 3
- conv_bc_bias: float32 [4, 256], P('section'), may hold values from -3 to 3
- inner_gain: float32 [4, 80, 64], P('section', 'tensor'), may hold values from 0.1 to 1.9
- w_out: bfloat16 [4, 80, 64, 2560], P('section', 'tensor'), may hold values from -0.078125 to 0.078125
- conv_x_state: bfloat16 [4, 64, 3, 80, 64], P('section', None, None, 'tensor'), may hold values from -6 to 6
- conv_bc_state: bfloat16 [4, 64, 3, 256], P('section'), may hold values from -6 to 6
- ssm_state: bfloat16 [4, 64, 80, 64, 128], P('section', None, 'tensor'), may hold values from -14 to 14
Outputs:
- section_hidden: bfloat16 [4, 64, 2560], P('section', None, 'tensor')
- conv_x_new: bfloat16 [4, 64, 3, 80, 64], P('section', None, None, 'tensor')
- conv_bc_new: bfloat16 [4, 64, 3, 256], P('section')
- ssm_new: bfloat16 [4, 64, 80, 64, 128], P('section', None, 'tensor')
All inputs are finite; a program needn't handle non-finite values.
Results may differ from a plain program's by a relative error of at most 0.02.
Values may be sent and summed in bfloat16 or wider, within the bound.
No kernel may reach another device: no remote copies, remote signals or barrier semaphores. Data moves between devices by JAX's collectives and lax.ppermute only.
A program may use at most 128 MiB of HBM per device.

v0:
```python
import jax
import jax.numpy as jnp
from jax import lax
from jax.sharding import PartitionSpec as P

epsilon = 1e-05


def shifted(value, axis, steps):
    count = lax.axis_size(axis)
    leading, last = (max(0, -steps), min(count, count - steps))
    return lax.ppermute(value, axis, [(source, source + steps) for source in range(leading, last)])


def mixer_core(
    normed,
    w_zx,
    w_bc,
    w_dt,
    dt_bias,
    a_log,
    d_skip,
    conv_x_weight,
    conv_x_bias,
    conv_bc_weight,
    conv_bc_bias,
    conv_x_state,
    conv_bc_state,
    ssm_state,
):
    row_count = normed.shape[0]
    model_width = w_zx.shape[0]
    head_count = w_zx.shape[1]
    head_size = w_zx.shape[2] // 2
    state_size = w_bc.shape[1] // 2
    both_parts = jnp.dot(
        normed,
        w_zx.reshape(model_width, head_count * 2 * head_size),
        preferred_element_type=jnp.float32,
    )
    both_parts = both_parts.reshape(row_count, head_count, 2 * head_size)
    gate_z = both_parts[:, :, :head_size]
    x_fresh = both_parts[:, :, head_size:].astype(jnp.bfloat16)
    bc_fresh = jnp.dot(normed, w_bc, preferred_element_type=jnp.float32).astype(jnp.bfloat16)
    dt_raw = jnp.dot(normed, w_dt, preferred_element_type=jnp.float32)
    x_window = jnp.concatenate([conv_x_state, x_fresh[:, None]], axis=1)
    bc_window = jnp.concatenate([conv_bc_state, bc_fresh[:, None]], axis=1)
    x_conv = jax.nn.silu(
        jnp.sum(x_window.astype(jnp.float32) * conv_x_weight[None], axis=1) + conv_x_bias[None]
    )
    bc_conv = jax.nn.silu(
        jnp.sum(bc_window.astype(jnp.float32) * conv_bc_weight[None], axis=1) + conv_bc_bias[None]
    )
    b_input = bc_conv[:, :state_size]
    c_output = bc_conv[:, state_size:]
    step_size = jax.nn.softplus(dt_raw + dt_bias[None])
    decay_rate = jnp.exp(-step_size * jnp.exp(a_log)[None])
    state_f = (
        decay_rate[:, :, None, None] * ssm_state.astype(jnp.float32)
        + (step_size[:, :, None] * x_conv)[:, :, :, None] * b_input[:, None, None, :]
    )
    y_out = jnp.sum(state_f * c_output[:, None, None, :], axis=-1) + d_skip[None, :, None] * x_conv
    gated_out = y_out * jax.nn.silu(gate_z)
    return (gated_out, x_window[:, 1:], bc_window[:, 1:], state_f.astype(jnp.bfloat16))


def put_rows(fresh, older, is_live):
    chosen = jnp.where(is_live, fresh, older)
    return chosen[None]


def shards(
    hidden_in,
    pre_gain,
    w_zx,
    w_bc,
    w_dt,
    dt_bias,
    a_log,
    d_skip,
    conv_x_weight,
    conv_x_bias,
    conv_bc_weight,
    conv_bc_bias,
    inner_gain,
    w_out,
    conv_x_state,
    conv_bc_state,
    ssm_state,
):
    section_count = lax.axis_size("section")
    tensor_count = lax.axis_size("tensor")
    section_at = lax.axis_index("section")
    tensor_at = lax.axis_index("tensor")
    stream_count = hidden_in.shape[0]
    share_cols = hidden_in.shape[1]
    blocks = 1
    block_rows = stream_count // blocks
    tick_count = blocks + section_count - 1
    source = lax.all_gather(hidden_in, "tensor", axis=1, tiled=True)
    carried_cols = source.shape[1]

    def advance(moment, carry):
        incoming, conv_x_buf, conv_bc_buf, ssm_buf, section_buf = carry
        which_block = moment - section_at
        is_live = jnp.logical_and(which_block >= 0, which_block < blocks)
        current = jnp.where(section_at == 0, source, incoming)
        conv_x_old = conv_x_buf[0]
        conv_bc_old = conv_bc_buf[0]
        ssm_old = ssm_buf[0]
        whole_rows = current
        wide = whole_rows.astype(jnp.float32)
        normed = (
            wide
            * lax.rsqrt(jnp.mean(wide * wide, axis=-1, keepdims=True) + epsilon)
            * pre_gain[0][None]
        ).astype(jnp.bfloat16)
        gated_out, conv_x_next, conv_bc_next, ssm_next = mixer_core(
            normed,
            w_zx[0],
            w_bc[0],
            w_dt[0],
            dt_bias[0],
            a_log[0],
            d_skip[0],
            conv_x_weight[0],
            conv_x_bias[0],
            conv_bc_weight[0],
            conv_bc_bias[0],
            conv_x_old,
            conv_bc_old,
            ssm_old,
        )
        local_squares = jnp.sum(gated_out * gated_out, axis=(1, 2))
        channel_total = gated_out.shape[1] * gated_out.shape[2] * tensor_count
        scaled_inner = (gated_out * inner_gain[0][None]).astype(jnp.bfloat16)
        local_heads = scaled_inner.shape[1] * scaled_inner.shape[2]
        partial_value = jnp.dot(
            scaled_inner.reshape(block_rows, local_heads),
            w_out[0].reshape(local_heads, w_out.shape[-1]),
            preferred_element_type=jnp.float32,
        )
        summed, summed_squares = lax.psum((partial_value, local_squares), "tensor")
        factor = lax.rsqrt(summed_squares / channel_total + epsilon)[:, None]
        current = (current.astype(jnp.float32) + summed * factor).astype(jnp.bfloat16)
        conv_x_buf = put_rows(conv_x_next, conv_x_old, is_live)
        conv_bc_buf = put_rows(conv_bc_next, conv_bc_old, is_live)
        ssm_buf = put_rows(ssm_next, ssm_old, is_live)
        own_share = lax.dynamic_slice_in_dim(current, tensor_at * share_cols, share_cols, 1)
        outgoing = shifted(current, "section", 1)
        section_old = section_buf[0]
        section_buf = put_rows(own_share, section_old, is_live)
        return (outgoing, conv_x_buf, conv_bc_buf, ssm_buf, section_buf)

    start_carry = (
        jnp.zeros((block_rows, carried_cols), jnp.bfloat16),
        conv_x_state,
        conv_bc_state,
        ssm_state,
        jnp.zeros((1, stream_count, share_cols), jnp.bfloat16),
    )
    final_carry = lax.fori_loop(0, tick_count, advance, start_carry)
    return (final_carry[4], final_carry[1], final_carry[2], final_carry[3])


def solution(mesh):
    placed = (
        P(None, "tensor"),
        P("section", None),
        P("section", None, "tensor", None),
        P("section", None, None),
        P("section", None, "tensor"),
        P("section", "tensor"),
        P("section", "tensor"),
        P("section", "tensor"),
        P("section", None, "tensor", None),
        P("section", "tensor", None),
        P("section", None, None),
        P("section", None),
        P("section", "tensor", None),
        P("section", "tensor", None, None),
        P("section", None, None, "tensor", None),
        P("section", None, None, None),
        P("section", None, "tensor", None, None),
    )
    return jax.shard_map(
        shards,
        mesh=mesh,
        in_specs=placed,
        out_specs=(
            P("section", None, "tensor"),
            P("section", None, None, "tensor", None),
            P("section", None, None, None),
            P("section", None, "tensor", None, None),
        ),
        check_vma=False,
    )
```

profile of v0, /device:TPU:3, one launch (start us, length us, event | category | flops | bytes accessed | tf_op | source)
XLA Modules:
  0.0 524.5 jit_solution(14849032680988920231)
XLA Ops:
  7.2 12.8 %copy.97 = bf16[1,64,10,64,128]{4,3,2,1,0:T(8,128)(2,1)} copy(bf16[1,64,10,64,128]{4,3,2,1,0:T(8,128)(2,1)} %param.35) | data formatting | bytes 20971520
  22.5 25.4 %all-gather = bf16[8,320,64]{1,2,0:T(8,128)(2,1)S(1)} all-gather(bf16[1,320,64]{1,2,0:T(8,128)(2,1)S(1)} %bitcast.123), channel_id=1, replica_groups=mesh['section'=4,'tensor'=8] {'tensor'}, dimensions={0}, use_global_device_ids=true | all-gather | bytes 368640 | tf_op jit(solution)/shard_map/all_gather | solution.py:100
  49.1 9.5 %copy.57 = bf16[1,2560,10,128]{1,3,2,0:T(8,128)(2,1)} copy(bf16[1,2560,10,128]{3,1,2,0:T(8,128)(2,1)} %param.21) | data formatting | bytes 13107200 | tf_op jit(solution)/shard_map/while | solution.py:162
  58.6 458.5 %while.23 = (s32[]{:T(128)}, bf16[64,2560]{1,0:T(8,128)(2,1)S(1)}, bf16[1,64,3,10,64]{4,1,3,2,0:T(8,128)(2,1)S(1)}, bf16[1,64,3,256]{3,1,2,0:T(8,128)(2,1)S(1)},...) while((s32[]{:T(128)}, bf16[64,2560]{1,0:T(8,128)(2,1)S(1)}, ...), condition=%wide.region_8.9_spmd, body=%wide.region_0.8_spmd.sunk | while | flops 784852800 | bytes 99354304 | solution.py:162
  59.7 1.2 multiply_exponential_fusion.2
  63.3 5.7 %fusion.67 = f32[64,10,128]{2,0,1:T(8,128)S(1)} fusion(bf16[1,2560,10,128]{1,3,2,0:T(8,128)(2,1)} %get-tuple-element.872, bf16[64,2560]{1,0:T(8,128)(2,1)S(1)} %get-tuple-element.800, f32[2560]{0:T(1024)S(1)} %reduce.2, f32[64]{0:T(128)S(1)} %add_rsqrt_fusion.4), kind=kOutput, calls=%fused_computation.9.clone.1 | convolution fusion | flops 420085760 | bytes 7219456 | tf_op jit(solution)/shard_map/while/body/eval_jaxpr/dot_general | solution.py:36
  71.3 13.7 %fusion.71 = f32[64,10,64]{2,1,0:T(8,128)S(1)} fusion(bf16[1,64,10,64,128]{4,3,2,1,0:T(8,128)(2,1)S(1)} %copy-done, f32[64,128]{1,0:T(8,128)S(1)} %get-tuple-element.802, f32[64,128]{1,0:T(8,128)S(1)} %get-tuple-element.803, f32[64,10,64]{2,1,0:T(8,128)S(1)} %copy.68, f32[64,10]{1,0:T(8,128)S(1)} %copy.69), kind=kLoop, calls=%fused_computation.5.clone.1 | loop fusion | flops 31416320 | bytes 10881536 | tf_op jit(solution)/shard_map/while/body/eval_jaxpr/reduce_sum | solution.py:62
  85.0 1.1 multiply_reduce_fusion.8
  86.3 3.5 fusion.72
  89.8 12.6 %fusion.76 = bf16[1,64,10,64,128]{4,3,2,1,0:T(8,128)(2,1)} fusion(bf16[1,64,10,64,128]{4,3,2,1,0:T(8,128)(2,1)} %get-tuple-element.838, f32[64,128]{1,0:T(8,128)S(1)} %get-tuple-element.803, f32[64,10,64]{2,1,0:T(8,128)S(1)} %copy.68, f32[64,10]{1,0:T(8,128)S(1)} %copy.69, pred[]{:T(512)S(6)} %and.12), kind=kLoop, calls=%fused_computation.8.clone.1 | loop fusion | flops 31457280 | bytes 21170688 | tf_op jit(solution)/shard_map/while/body/eval_jaxpr/jit(_where)/select_n | solution.py:68
  102.4 17.3 %psum.29 = f32[64]{0:T(128)S(1)} all-reduce(f32[64]{0:T(128)S(1)} %get-tuple-element.807), channel_id=1, replica_groups=mesh['section'=4,'tensor'=8] {'tensor'}, use_global_device_ids=true, to_apply=%region_7.7 | all-reduce | flops 64 | bytes 512 | tf_op jit(solution)/shard_map/while/body/eval_jaxpr/psum | solution.py:143
  119.8 49.1 %all-reduce.2.cloned.1.call-done = f32[64,2560]{1,0:T(8,128)} async-done(((f32[64,2560]{1,0:T(8,128)}), f32[64,2560]{1,0:T(8,128)}) %all-reduce.2.cloned.1.call-update) | async-done | bytes 655376 | tf_op jit(solution)/shard_map/while/body/eval_jaxpr/psum | solution.py:143
  168.9 1.2 fusion.73
  170.2 1.3 collective-permute-start
  171.6 3.9 collective-permute-done
  176.5 1.2 multiply_exponential_fusion.2
  180.1 5.7 %fusion.67 = f32[64,10,128]{2,0,1:T(8,128)S(1)} fusion(bf16[1,2560,10,128]{1,3,2,0:T(8,128)(2,1)} %get-tuple-element.872, bf16[64,2560]{1,0:T(8,128)(2,1)S(1)} %get-tuple-element.800, f32[2560]{0:T(1024)S(1)} %reduce.2, f32[64]{0:T(128)S(1)} %add_rsqrt_fusion.4), kind=kOutput, calls=%fused_computation.9.clone.1 | convolution fusion | flops 420085760 | bytes 7219456 | tf_op jit(solution)/shard_map/while/body/eval_jaxpr/dot_general | solution.py:36
  188.1 13.7 %fusion.71 = f32[64,10,64]{2,1,0:T(8,128)S(1)} fusion(bf16[1,64,10,64,128]{4,3,2,1,0:T(8,128)(2,1)S(1)} %copy-done, f32[64,128]{1,0:T(8,128)S(1)} %get-tuple-element.802, f32[64,128]{1,0:T(8,128)S(1)} %get-tuple-element.803, f32[64,10,64]{2,1,0:T(8,128)S(1)} %copy.68, f32[64,10]{1,0:T(8,128)S(1)} %copy.69), kind=kLoop, calls=%fused_computation.5.clone.1 | loop fusion | flops 31416320 | bytes 10881536 | tf_op jit(solution)/shard_map/while/body/eval_jaxpr/reduce_sum | solution.py:62
  201.8 1.1 multiply_reduce_fusion.8
  203.1 3.5 fusion.72
  206.6 12.7 %fusion.76 = bf16[1,64,10,64,128]{4,3,2,1,0:T(8,128)(2,1)} fusion(bf16[1,64,10,64,128]{4,3,2,1,0:T(8,128)(2,1)} %get-tuple-element.838, f32[64,128]{1,0:T(8,128)S(1)} %get-tuple-element.803, f32[64,10,64]{2,1,0:T(8,128)S(1)} %copy.68, f32[64,10]{1,0:T(8,128)S(1)} %copy.69, pred[]{:T(512)S(6)} %and.12), kind=kLoop, calls=%fused_computation.8.clone.1 | loop fusion | flops 31457280 | bytes 21170688 | tf_op jit(solution)/shard_map/while/body/eval_jaxpr/jit(_where)/select_n | solution.py:68
  219.3 16.1 %psum.29 = f32[64]{0:T(128)S(1)} all-reduce(f32[64]{0:T(128)S(1)} %get-tuple-element.807), channel_id=1, replica_groups=mesh['section'=4,'tensor'=8] {'tensor'}, use_global_device_ids=true, to_apply=%region_7.7 | all-reduce | flops 64 | bytes 512 | tf_op jit(solution)/shard_map/while/body/eval_jaxpr/psum | solution.py:143
  235.6 47.2 %all-reduce.2.cloned.1.call-done = f32[64,2560]{1,0:T(8,128)} async-done(((f32[64,2560]{1,0:T(8,128)}), f32[64,2560]{1,0:T(8,128)}) %all-reduce.2.cloned.1.call-update) | async-done | bytes 655376 | tf_op jit(solution)/shard_map/while/body/eval_jaxpr/psum | solution.py:143
  282.8 1.2 fusion.73
  284.0 1.3 collective-permute-start
  285.5 3.9 collective-permute-done
  290.4 1.2 multiply_exponential_fusion.2
  294.0 5.7 %fusion.67 = f32[64,10,128]{2,0,1:T(8,128)S(1)} fusion(bf16[1,2560,10,128]{1,3,2,0:T(8,128)(2,1)} %get-tuple-element.872, bf16[64,2560]{1,0:T(8,128)(2,1)S(1)} %get-tuple-element.800, f32[2560]{0:T(1024)S(1)} %reduce.2, f32[64]{0:T(128)S(1)} %add_rsqrt_fusion.4), kind=kOutput, calls=%fused_computation.9.clone.1 | convolution fusion | flops 420085760 | bytes 7219456 | tf_op jit(solution)/shard_map/while/body/eval_jaxpr/dot_general | solution.py:36
  302.0 13.7 %fusion.71 = f32[64,10,64]{2,1,0:T(8,128)S(1)} fusion(bf16[1,64,10,64,128]{4,3,2,1,0:T(8,128)(2,1)S(1)} %copy-done, f32[64,128]{1,0:T(8,128)S(1)} %get-tuple-element.802, f32[64,128]{1,0:T(8,128)S(1)} %get-tuple-element.803, f32[64,10,64]{2,1,0:T(8,128)S(1)} %copy.68, f32[64,10]{1,0:T(8,128)S(1)} %copy.69), kind=kLoop, calls=%fused_computation.5.clone.1 | loop fusion | flops 31416320 | bytes 10881536 | tf_op jit(solution)/shard_map/while/body/eval_jaxpr/reduce_sum | solution.py:62
  315.7 1.1 multiply_reduce_fusion.8
  317.0 3.5 fusion.72
  320.5 12.7 %fusion.76 = bf16[1,64,10,64,128]{4,3,2,1,0:T(8,128)(2,1)} fusion(bf16[1,64,10,64,128]{4,3,2,1,0:T(8,128)(2,1)} %get-tuple-element.838, f32[64,128]{1,0:T(8,128)S(1)} %get-tuple-element.803, f32[64,10,64]{2,1,0:T(8,128)S(1)} %copy.68, f32[64,10]{1,0:T(8,128)S(1)} %copy.69, pred[]{:T(512)S(6)} %and.12), kind=kLoop, calls=%fused_computation.8.clone.1 | loop fusion | flops 31457280 | bytes 21170688 | tf_op jit(solution)/shard_map/while/body/eval_jaxpr/jit(_where)/select_n | solution.py:68
  333.2 16.1 %psum.29 = f32[64]{0:T(128)S(1)} all-reduce(f32[64]{0:T(128)S(1)} %get-tuple-element.807), channel_id=1, replica_groups=mesh['section'=4,'tensor'=8] {'tensor'}, use_global_device_ids=true, to_apply=%region_7.7 | all-reduce | flops 64 | bytes 512 | tf_op jit(solution)/shard_map/while/body/eval_jaxpr/psum | solution.py:143
  349.4 47.3 %all-reduce.2.cloned.1.call-done = f32[64,2560]{1,0:T(8,128)} async-done(((f32[64,2560]{1,0:T(8,128)}), f32[64,2560]{1,0:T(8,128)}) %all-reduce.2.cloned.1.call-update) | async-done | bytes 655376 | tf_op jit(solution)/shard_map/while/body/eval_jaxpr/psum | solution.py:143
  396.7 1.2 fusion.73
  397.9 1.3 collective-permute-start
  399.4 3.9 collective-permute-done
  404.3 1.2 multiply_exponential_fusion.2
  407.9 5.7 %fusion.67 = f32[64,10,128]{2,0,1:T(8,128)S(1)} fusion(bf16[1,2560,10,128]{1,3,2,0:T(8,128)(2,1)} %get-tuple-element.872, bf16[64,2560]{1,0:T(8,128)(2,1)S(1)} %get-tuple-element.800, f32[2560]{0:T(1024)S(1)} %reduce.2, f32[64]{0:T(128)S(1)} %add_rsqrt_fusion.4), kind=kOutput, calls=%fused_computation.9.clone.1 | convolution fusion | flops 420085760 | bytes 7219456 | tf_op jit(solution)/shard_map/while/body/eval_jaxpr/dot_general | solution.py:36
  415.9 13.7 %fusion.71 = f32[64,10,64]{2,1,0:T(8,128)S(1)} fusion(bf16[1,64,10,64,128]{4,3,2,1,0:T(8,128)(2,1)S(1)} %copy-done, f32[64,128]{1,0:T(8,128)S(1)} %get-tuple-element.802, f32[64,128]{1,0:T(8,128)S(1)} %get-tuple-element.803, f32[64,10,64]{2,1,0:T(8,128)S(1)} %copy.68, f32[64,10]{1,0:T(8,128)S(1)} %copy.69), kind=kLoop, calls=%fused_computation.5.clone.1 | loop fusion | flops 31416320 | bytes 10881536 | tf_op jit(solution)/shard_map/while/body/eval_jaxpr/reduce_sum | solution.py:62
  429.6 1.1 multiply_reduce_fusion.8
  430.9 3.5 fusion.72
  434.4 12.7 %fusion.76 = bf16[1,64,10,64,128]{4,3,2,1,0:T(8,128)(2,1)} fusion(bf16[1,64,10,64,128]{4,3,2,1,0:T(8,128)(2,1)} %get-tuple-element.838, f32[64,128]{1,0:T(8,128)S(1)} %get-tuple-element.803, f32[64,10,64]{2,1,0:T(8,128)S(1)} %copy.68, f32[64,10]{1,0:T(8,128)S(1)} %copy.69, pred[]{:T(512)S(6)} %and.12), kind=kLoop, calls=%fused_computation.8.clone.1 | loop fusion | flops 31457280 | bytes 21170688 | tf_op jit(solution)/shard_map/while/body/eval_jaxpr/jit(_where)/select_n | solution.py:68
  447.1 16.1 %psum.29 = f32[64]{0:T(128)S(1)} all-reduce(f32[64]{0:T(128)S(1)} %get-tuple-element.807), channel_id=1, replica_groups=mesh['section'=4,'tensor'=8] {'tensor'}, use_global_device_ids=true, to_apply=%region_7.7 | all-reduce | flops 64 | bytes 512 | tf_op jit(solution)/shard_map/while/body/eval_jaxpr/psum | solution.py:143
  463.3 47.2 %all-reduce.2.cloned.1.call-done = f32[64,2560]{1,0:T(8,128)} async-done(((f32[64,2560]{1,0:T(8,128)}), f32[64,2560]{1,0:T(8,128)}) %all-reduce.2.cloned.1.call-update) | async-done | bytes 655376 | tf_op jit(solution)/shard_map/while/body/eval_jaxpr/psum | solution.py:143
  510.6 1.2 fusion.73
  511.8 1.3 collective-permute-start
  513.3 3.9 collective-permute-done
  (142 shorter events, 28.8 us)
Async XLA Ops:
  7.2 15.3 %copy-start.8 = (bf16[64,320]{1,0:T(8,128)(2,1)S(1)}, bf16[64,320]{1,0:T(8,128)(2,1)}, u32[]{:S(2)}) copy-start(bf16[64,320]{1,0:T(8,128)(2,1)} %param.19) | copy-start | bytes 122884
  7.2 12.9 %copy-start.13 = (f32[1,10]{1,0:T(1,128)S(1)}, f32[1,10]{1,0:T(1,128)}, u32[]{:S(2)}) copy-start(f32[1,10]{1,0:T(1,128)} %param.25) | copy-start | bytes 124
  7.2 14.7 %copy-start.9 = (f32[1,4,10,64]{3,1,2,0:T(4,128)S(1)}, f32[1,4,10,64]{3,1,2,0:T(4,128)}, u32[]{:S(2)}) copy-start(f32[1,4,10,64]{3,1,2,0:T(4,128)} %param.27) | copy-start | bytes 30724
  7.2 13.5 %copy-start.11 = (f32[1,10,64]{2,0,1:T(1,128)S(1)}, f32[1,10,64]{2,0,1:T(1,128)}, u32[]{:S(2)}) copy-start(f32[1,10,64]{2,0,1:T(1,128)} %param.28) | copy-start | bytes 7684
  7.2 14.1 %copy-start.12 = (f32[1,10,64]{2,0,1:T(1,128)S(1)}, f32[1,10,64]{2,0,1:T(1,128)}, u32[]{:S(2)}) copy-start(f32[1,10,64]{2,0,1:T(1,128)} %param.31) | copy-start | bytes 7684
  20.1 38.5 %copy-start.1 = (bf16[1,2560,256]{2,1,0:T(8,128)(2,1)S(1)}, bf16[1,2560,256]{2,1,0:T(8,128)(2,1)}, u32[]{:S(2)}) copy-start(bf16[1,2560,256]{2,1,0:T(8,128)(2,1)} %param.22) | copy-start | bytes 3932164
  20.1 38.6 %copy-start.3 = (bf16[1,64,3,10,64]{4,1,3,2,0:T(8,128)(2,1)S(1)}, bf16[1,64,3,10,64]{4,1,3,2,0:T(8,128)(2,1)}, u32[]{:S(2)}) copy-start(bf16[1,64,3,10,64]{4,1,3,2,0:T(8,128)(2,1)} %param.33) | copy-start | bytes 737284
  20.1 38.6 %copy-start.5 = (bf16[1,64,3,256]{3,1,2,0:T(8,128)(2,1)S(1)}, bf16[1,64,3,256]{3,1,2,0:T(8,128)(2,1)}, u32[]{:S(2)}) copy-start(bf16[1,64,3,256]{3,1,2,0:T(8,128)(2,1)} %param.34) | copy-start | bytes 294916
  58.6 110.3 %all-reduce.2.cloned.1.call-start = ((), (), s32[]{:S(2)}) async-start(), calls=%async_computation | async-start | bytes 1310720 | tf_op jit(solution)/shard_map/while/body/eval_jaxpr/psum | solution.py:143
  61.0 10.3 %copy-start = (bf16[1,64,10,64,128]{4,3,2,1,0:T(8,128)(2,1)S(1)}, bf16[1,64,10,64,128]{4,3,2,1,0:T(8,128)(2,1)}, u32[]{:S(2)}) copy-start(bf16[1,64,10,64,128]{4,3,2,1,0:T(8,128)(2,1)} %get-tuple-element.838) | copy-start | bytes 31457284 | tf_op jit(solution)/shard_map/while
  63.3 21.7 %copy-start.10 = (f32[1,10]{1,0:T(1,128)S(1)}, f32[1,10]{1,0:T(1,128)}, u32[]{:S(2)}) copy-start(f32[1,10]{1,0:T(1,128)} %get-tuple-element.878) | copy-start | bytes 124 | tf_op jit(solution)/shard_map/while
  63.3 22.7 %copy-start.7 = (f32[1,10,64]{2,1,0:T(8,128)S(1)}, f32[1,10,64]{2,1,0:T(8,128)}, u32[]{:S(2)}) copy-start(f32[1,10,64]{2,1,0:T(8,128)} %get-tuple-element.879) | copy-start | bytes 7684 | tf_op jit(solution)/shard_map/while
  170.2 5.3 %collective-permute-start = (bf16[64,2560]{1,0:T(8,128)(2,1)S(1)}, bf16[64,2560]{1,0:T(8,128)(2,1)S(1)}, u32[]{:S(2)}, u32[]{:S(2)}) collective-permute-start(bf16[64,2560]{1,0:T(8,128)(2,1)S(1)} %fusion.73), channel_id=1, source_target_pairs={{0,8},{8,16},{16,24},{1,9},{9,17},{17,25},{2,10},{10,18},{18,26},{... | collective-permute-start | bytes 983048 | tf_op jit(solution)/shard_map/while/body/eval_jaxpr/ppermute | solution.py:12
  175.5 107.3 %all-reduce.2.cloned.1.call-start = ((), (), s32[]{:S(2)}) async-start(), calls=%async_computation | async-start | bytes 1310720 | tf_op jit(solution)/shard_map/while/body/eval_jaxpr/psum | solution.py:143
  177.8 10.3 %copy-start = (bf16[1,64,10,64,128]{4,3,2,1,0:T(8,128)(2,1)S(1)}, bf16[1,64,10,64,128]{4,3,2,1,0:T(8,128)(2,1)}, u32[]{:S(2)}) copy-start(bf16[1,64,10,64,128]{4,3,2,1,0:T(8,128)(2,1)} %get-tuple-element.838) | copy-start | bytes 31457284 | tf_op jit(solution)/shard_map/while
  180.1 21.7 %copy-start.10 = (f32[1,10]{1,0:T(1,128)S(1)}, f32[1,10]{1,0:T(1,128)}, u32[]{:S(2)}) copy-start(f32[1,10]{1,0:T(1,128)} %get-tuple-element.878) | copy-start | bytes 124 | tf_op jit(solution)/shard_map/while
  180.1 22.7 %copy-start.7 = (f32[1,10,64]{2,1,0:T(8,128)S(1)}, f32[1,10,64]{2,1,0:T(8,128)}, u32[]{:S(2)}) copy-start(f32[1,10,64]{2,1,0:T(8,128)} %get-tuple-element.879) | copy-start | bytes 7684 | tf_op jit(solution)/shard_map/while
  284.0 5.3 %collective-permute-start = (bf16[64,2560]{1,0:T(8,128)(2,1)S(1)}, bf16[64,2560]{1,0:T(8,128)(2,1)S(1)}, u32[]{:S(2)}, u32[]{:S(2)}) collective-permute-start(bf16[64,2560]{1,0:T(8,128)(2,1)S(1)} %fusion.73), channel_id=1, source_target_pairs={{0,8},{8,16},{16,24},{1,9},{9,17},{17,25},{2,10},{10,18},{18,26},{... | collective-permute-start | bytes 983048 | tf_op jit(solution)/shard_map/while/body/eval_jaxpr/ppermute | solution.py:12
  289.4 107.3 %all-reduce.2.cloned.1.call-start = ((), (), s32[]{:S(2)}) async-start(), calls=%async_computation | async-start | bytes 1310720 | tf_op jit(solution)/shard_map/while/body/eval_jaxpr/psum | solution.py:143
  291.7 10.3 %copy-start = (bf16[1,64,10,64,128]{4,3,2,1,0:T(8,128)(2,1)S(1)}, bf16[1,64,10,64,128]{4,3,2,1,0:T(8,128)(2,1)}, u32[]{:S(2)}) copy-start(bf16[1,64,10,64,128]{4,3,2,1,0:T(8,128)(2,1)} %get-tuple-element.838) | copy-start | bytes 31457284 | tf_op jit(solution)/shard_map/while
  294.0 21.7 %copy-start.10 = (f32[1,10]{1,0:T(1,128)S(1)}, f32[1,10]{1,0:T(1,128)}, u32[]{:S(2)}) copy-start(f32[1,10]{1,0:T(1,128)} %get-tuple-element.878) | copy-start | bytes 124 | tf_op jit(solution)/shard_map/while
  294.0 22.7 %copy-start.7 = (f32[1,10,64]{2,1,0:T(8,128)S(1)}, f32[1,10,64]{2,1,0:T(8,128)}, u32[]{:S(2)}) copy-start(f32[1,10,64]{2,1,0:T(8,128)} %get-tuple-element.879) | copy-start | bytes 7684 | tf_op jit(solution)/shard_map/while
  397.9 5.3 %collective-permute-start = (bf16[64,2560]{1,0:T(8,128)(2,1)S(1)}, bf16[64,2560]{1,0:T(8,128)(2,1)S(1)}, u32[]{:S(2)}, u32[]{:S(2)}) collective-permute-start(bf16[64,2560]{1,0:T(8,128)(2,1)S(1)} %fusion.73), channel_id=1, source_target_pairs={{0,8},{8,16},{16,24},{1,9},{9,17},{17,25},{2,10},{10,18},{18,26},{... | collective-permute-start | bytes 983048 | tf_op jit(solution)/shard_map/while/body/eval_jaxpr/ppermute | solution.py:12
  403.3 107.3 %all-reduce.2.cloned.1.call-start = ((), (), s32[]{:S(2)}) async-start(), calls=%async_computation | async-start | bytes 1310720 | tf_op jit(solution)/shard_map/while/body/eval_jaxpr/psum | solution.py:143
  405.6 10.3 %copy-start = (bf16[1,64,10,64,128]{4,3,2,1,0:T(8,128)(2,1)S(1)}, bf16[1,64,10,64,128]{4,3,2,1,0:T(8,128)(2,1)}, u32[]{:S(2)}) copy-start(bf16[1,64,10,64,128]{4,3,2,1,0:T(8,128)(2,1)} %get-tuple-element.838) | copy-start | bytes 31457284 | tf_op jit(solution)/shard_map/while
  407.9 21.7 %copy-start.10 = (f32[1,10]{1,0:T(1,128)S(1)}, f32[1,10]{1,0:T(1,128)}, u32[]{:S(2)}) copy-start(f32[1,10]{1,0:T(1,128)} %get-tuple-element.878) | copy-start | bytes 124 | tf_op jit(solution)/shard_map/while
  407.9 22.7 %copy-start.7 = (f32[1,10,64]{2,1,0:T(8,128)S(1)}, f32[1,10,64]{2,1,0:T(8,128)}, u32[]{:S(2)}) copy-start(f32[1,10,64]{2,1,0:T(8,128)} %get-tuple-element.879) | copy-start | bytes 7684 | tf_op jit(solution)/shard_map/while
  511.8 5.3 %collective-permute-start = (bf16[64,2560]{1,0:T(8,128)(2,1)S(1)}, bf16[64,2560]{1,0:T(8,128)(2,1)S(1)}, u32[]{:S(2)}, u32[]{:S(2)}) collective-permute-start(bf16[64,2560]{1,0:T(8,128)(2,1)S(1)} %fusion.73), channel_id=1, source_target_pairs={{0,8},{8,16},{16,24},{1,9},{9,17},{17,25},{2,10},{10,18},{18,26},{... | collective-permute-start | bytes 983048 | tf_op jit(solution)/shard_map/while/body/eval_jaxpr/ppermute | solution.py:12
  517.2 0.8 copy-start.2
  517.2 0.8 copy-start.4
  517.2 0.8 copy-start.6
Sparse Core Ops, SparseCore 0:
  89.9 78.9 all-reduce.1
  206.7 76.0 all-reduce.1
  320.6 76.0 all-reduce.1
  434.5 76.0 all-reduce.1
where the time goes:
time: 531 us; the launch traced here: 525 us
  waiting for transfers between devices  207 us (39%)
  other arithmetic  135 us (25%)
  blocking collectives  90.9 us (17%)
  matrix products  42.9 us (8%)
  local copies, waits for them, and re-layouts  29.3 us (6%)
  between operations  13.8 us (3%)
    psum x4, waiting for transfers between devices, advance(): summed, summed_squares = lax.psum((partial_value, local_squares), 'tensor')  191 us
    psum x4, blocking collectives, advance(): summed, summed_squares = lax.psum((partial_value, local_squares), 'tensor')  65.6 us
    reduce_sum x4, other arithmetic, mixer_core(): jnp.sum(state_f * c_output[:, None, None, :], axis=-1)  54.8 us
    select_n x4, other arithmetic, put_rows(): chosen = jnp.where(is_live, fresh, older)  50.9 us
    all_gather x1, blocking collectives, shards(): source = lax.all_gather(hidden_in, 'tensor', axis=1, tiled=True)  25.4 us
    dot_general x4, matrix products, mixer_core(): jnp.dot(normed, w_zx.reshape(model_width, head_count * 2 * head_size), pr...  22.7 us
    ppermute x4, waiting for transfers between devices, shifted(): lax.ppermute(value, axis, [(source, source + steps) for source in range(l...  15.7 us
    unnamed x24, local copies, waits for them, and re-layouts  14.7 us
  transfers between devices with their start and end apart: 8, of which 8 were waited for; matrix products, arithmetic and copies ran while one was open for 10% of the time, Pallas kernels for 0%

commit v1 on v0

v1 whole, which is shorter than its diff:
```python
import jax
import jax.numpy as jnp
from jax import lax
from jax.sharding import PartitionSpec as P

epsilon = 1e-05


def gather_shares(share):
    count = lax.axis_size("tensor")
    spread = jnp.broadcast_to(share[None], (count,) + share.shape)
    return lax.all_to_all(spread, "tensor", 0, 0, tiled=True)


def shards(
    hidden_in,
    pre_gain,
    w_zx,
    w_bc,
    w_dt,
    dt_bias,
    a_log,
    d_skip,
    conv_x_weight,
    conv_x_bias,
    conv_bc_weight,
    conv_bc_bias,
    inner_gain,
    w_out,
    conv_x_state,
    conv_bc_state,
    ssm_state,
):
    section_count = lax.axis_size("section")
    tensor_count = lax.axis_size("tensor")
    section_at = lax.axis_index("section")
    streams, share_cols = hidden_in.shape
    width = w_zx.shape[1]
    heads = w_zx.shape[2]
    head_size = w_zx.shape[3] // 2
    state_size = w_bc.shape[2] // 2
    inner = heads * head_size
    all_channels = inner * tensor_count
    w_heads = jnp.transpose(w_zx[0], (1, 0, 2))
    state = ssm_state[0]

    def live(share, saved):
        shares = gather_shares(share)
        full = jnp.transpose(shares, (1, 0, 2)).reshape(streams, width)
        wide = full.astype(jnp.float32)
        normed = (
            wide
            * lax.rsqrt(jnp.mean(wide * wide, axis=-1, keepdims=True) + epsilon)
            * pre_gain[0][None]
        ).astype(jnp.bfloat16)
        zx = jnp.einsum("sd,hdc->shc", normed, w_heads, preferred_element_type=jnp.float32)
        gate_z = zx[:, :, :head_size]
        x_fresh = zx[:, :, head_size:].astype(jnp.bfloat16)
        bc_fresh = jnp.dot(normed, w_bc[0], preferred_element_type=jnp.float32).astype(jnp.bfloat16)
        dt_raw = jnp.dot(normed, w_dt[0], preferred_element_type=jnp.float32)
        x_window = jnp.concatenate([conv_x_state[0], x_fresh[:, None]], axis=1)
        bc_window = jnp.concatenate([conv_bc_state[0], bc_fresh[:, None]], axis=1)
        x_conv = jax.nn.silu(
            jnp.sum(x_window.astype(jnp.float32) * conv_x_weight[0][None], axis=1)
            + conv_x_bias[0][None]
        )
        bc_conv = jax.nn.silu(
            jnp.sum(bc_window.astype(jnp.float32) * conv_bc_weight[0][None], axis=1)
            + conv_bc_bias[0][None]
        )
        b_input = bc_conv[:, :state_size]
        c_output = bc_conv[:, state_size:]
        step_size = jax.nn.softplus(dt_raw + dt_bias[0][None])
        decay = jnp.exp(-step_size * jnp.exp(a_log[0])[None])
        stepped = step_size[:, :, None] * x_conv
        old_part = jnp.sum(state.astype(jnp.float32) * c_output[:, None, None, :], axis=-1)
        overlap = jnp.sum(b_input * c_output, axis=-1)
        y_out = (
            decay[:, :, None] * old_part
            + stepped * overlap[:, None, None]
            + d_skip[0][None, :, None] * x_conv
        )
        gated = y_out * jax.nn.silu(gate_z)
        squares = jnp.sum(gated * gated, axis=(1, 2))
        scaled = (gated * inner_gain[0][None]).astype(jnp.bfloat16)
        partial = jnp.dot(
            scaled.reshape(streams, inner),
            w_out[0].reshape(inner, width),
            preferred_element_type=jnp.float32,
        )
        pieces = partial.astype(jnp.bfloat16).reshape(streams, tensor_count, share_cols)
        pieces = jnp.transpose(pieces, (1, 0, 2))
        high = squares.astype(jnp.bfloat16)
        low = (squares - high.astype(jnp.float32)).astype(jnp.bfloat16)
        tail = jnp.stack([high, low], axis=1)[None]
        tail = jnp.broadcast_to(tail, (tensor_count, streams, 2))
        sent = jnp.concatenate([pieces, tail], axis=2)
        got = lax.all_to_all(sent, "tensor", 0, 0, tiled=True).astype(jnp.float32)
        total = jnp.sum(got, axis=0)
        squares_all = total[:, share_cols] + total[:, share_cols + 1]
        factor = lax.rsqrt(squares_all / all_channels + epsilon)[:, None]
        fresh = (share.astype(jnp.float32) + total[:, :share_cols] * factor).astype(jnp.bfloat16)
        return fresh, (x_fresh, bc_fresh, stepped, b_input, decay)

    saved = (
        jnp.zeros((streams, heads, head_size), jnp.bfloat16),
        jnp.zeros((streams, 2 * state_size), jnp.bfloat16),
        jnp.zeros((streams, heads, head_size), jnp.float32),
        jnp.zeros((streams, state_size), jnp.float32),
        jnp.zeros((streams, heads), jnp.float32),
    )
    incoming = hidden_in
    section_share = jnp.zeros_like(hidden_in)
    for tick in range(section_count):
        is_live = section_at == tick
        section_share, saved = lax.cond(
            is_live,
            lambda share, kept, old: live(share, old),
            lambda share, kept, old: (kept, old),
            incoming,
            section_share,
            saved,
        )
        if tick + 1 < section_count:
            ring = [(at, (at + 1) % section_count) for at in range(section_count)]
            incoming = lax.ppermute(section_share, "section", ring)
    x_fresh, bc_fresh, stepped, b_input, decay = saved
    state_f = (
        decay[:, :, None, None] * state.astype(jnp.float32)
        + stepped[:, :, :, None] * b_input[:, None, None, :]
    )
    conv_x_new = jnp.concatenate([conv_x_state[0][:, 1:], x_fresh[:, None]], axis=1)
    conv_bc_new = jnp.concatenate([conv_bc_state[0][:, 1:], bc_fresh[:, None]], axis=1)
    return (
        section_share[None],
        conv_x_new[None],
        conv_bc_new[None],
        state_f.astype(jnp.bfloat16)[None],
    )


def solution(mesh):
    placed = (
        P(None, "tensor"),
        P("section", None),
        P("section", None, "tensor", None),
        P("section", None, None),
        P("section", None, "tensor"),
        P("section", "tensor"),
        P("section", "tensor"),
        P("section", "tensor"),
        P("section", None, "tensor", None),
        P("section", "tensor", None),
        P("section", None, None),
        P("section", None),
        P("section", "tensor", None),
        P("section", "tensor", None, None),
        P("section", None, None, "tensor", None),
        P("section", None, None, None),
        P("section", None, "tensor", None, None),
    )
    return jax.shard_map(
        shards,
        mesh=mesh,
        in_specs=placed,
        out_specs=(
            P("section", None, "tensor"),
            P("section", None, None, "tensor", None),
            P("section", None, None, None),
            P("section", None, "tensor", None, None),
        ),
        check_vma=False,
    )
```

time: 531 us -> 242 us (0.46); the launches traced: 525 us -> 241 us
  waiting for transfers between devices: 207 us -> 58.5 us
  starting transfers between devices: 5.22 us -> 112 us
  other arithmetic: 135 us -> 28.8 us
  blocking collectives: 90.9 us -> 11.4 us
  matrix products: 42.9 us -> 9.73 us
  between operations: 13.8 us -> 0.65 us
  local copies, waits for them, and re-layouts: 29.3 us -> 19.7 us
    psum x4 -> x0, waiting for transfers between devices: 191 us -> none  [advance(): summed, summed_squares = lax.psum((partial_value, local_squares), 'tensor')]
    ppermute x4 -> x3, starting transfers between devices: 5.17 us -> 108 us  [shards(): incoming = lax.ppermute(section_share, 'section', ring)]
    psum x4 -> x0, blocking collectives: 65.6 us -> none  [advance(): summed, summed_squares = lax.psum((partial_value, local_squares), 'tensor')]
    reduce_sum x20 -> x7, other arithmetic: 67.7 us -> 10.4 us  [the longest x1 8.54 us: live(): jnp.sum(state.astype(jnp.float32) * c_output[:, None, None, :], axis=-1)]
    select_n x4 -> x0, other arithmetic: 50.9 us -> none  [put_rows(): chosen = jnp.where(is_live, fresh, older)]
    ppermute x4 -> x3, waiting for transfers between devices: 15.7 us -> 56.6 us  [shards(): incoming = lax.ppermute(section_share, 'section', ring)]
    dot_general x16 -> x4, matrix products: 42.9 us -> 9.73 us  [the longest x1 4.16 us: live(): jnp.einsum('sd,hdc->shc', normed, w_heads, preferred_element_type=jnp.flo...]
    all_gather x1 -> x0, blocking collectives: 25.4 us -> none  [shards(): source = lax.all_gather(hidden_in, 'tensor', axis=1, tiled=True)]
  transfers between devices with their start and end apart: 8 -> 4, of which waited for: 8 -> 4; matrix products, arithmetic and copies ran while one was open for 10% -> 4% of each run, Pallas kernels for 0% -> 0%
where the time goes in v1:
time: 242 us; the launch traced here: 241 us
  starting transfers between devices  112 us (46%)
  waiting for transfers between devices  58.5 us (24%)
  other arithmetic  28.8 us (12%)
  local copies, waits for them, and re-layouts  19.7 us (8%)
  blocking collectives  11.4 us (5%)
  matrix products  9.73 us (4%)
    ppermute x3, starting transfers between devices, shards(): incoming = lax.ppermute(section_share, 'section', ring)  108 us
    ppermute x3, waiting for transfers between devices, shards(): incoming = lax.ppermute(section_share, 'section', ring)  56.6 us
    all_to_all x1, blocking collectives, live(): got = lax.all_to_all(sent, 'tensor', 0, 0, tiled=True).astype(jnp.float32)  11.4 us
    convert_element_type x1, other arithmetic, shards(): state_f.astype(jnp.bfloat16)[None]  10.4 us
    reduce_sum x1, other arithmetic, live(): jnp.sum(state.astype(jnp.float32) * c_output[:, None, None, :], axis=-1)  8.54 us
  transfers between devices with their start and end apart: 4, of which 4 were waited for; matrix products, arithmetic and copies ran while one was open for 4% of the time, Pallas kernels for 0%

profile of v1, /device:TPU:3, one launch (start us, length us, event | category | flops | bytes accessed | tf_op | source)
XLA Modules:
  0.0 240.9 jit_solution(17387687312889299391)
XLA Ops:
  0.6 3.2 %conditional.4 = (bf16[64,320]{1,0:T(8,128)(2,1)}, bf16[64,10,64]{2,0,1:T(8,128)(2,1)S(1)}, bf16[64,256]{1,0:T(8,128)(2,1)}, f32[64,10,64]{2,0,1:T(8,128)}, f32[64,128]{1,0:T(8,128)}, /*index=5*/f32[64,10]{0,1:T(8,128)}) conditional(s32[]{:T(128)} %convert_element_type.359, () %tuple.44, (bf16[64,320]{1,0:T(8,128)(2,1)}, f32[1,2560]{1,0:T(1,128)}, ...), branch_computations={%region_0.0_spmd, %region_1.9_spmd} | conditional | flops 736944576 | bytes 56801684 | solution.py:116
  0.6 0.8 broadcast_in_dim.62
  1.4 0.6 broadcast_in_dim.59
  2.1 0.6 broadcast_in_dim.61
  2.7 0.6 broadcast_in_dim.80
  3.3 0.6 broadcast_in_dim.81
  3.9 55.8 %collective-permute-start = (bf16[64,320]{1,0:T(8,128)(2,1)}, bf16[64,320]{1,0:T(8,128)(2,1)S(1)}, u32[]{:S(2)}, u32[]{:S(2)}) collective-permute-start(bf16[64,320]{1,0:T(8,128)(2,1)} %get-tuple-element.273), channel_id=1, source_target_pairs={{0,8},{8,16},{16,24},{24,0},{1,9},{9,17},{17,25},{25,1},{2,10},{10... | collective-permute-start | bytes 122888 | tf_op jit(solution)/shard_map/ppermute | solution.py:126
  59.7 1.5 collective-permute-done
  61.2 2.2 collective-permute-start.1
  63.4 1.5 collective-permute-done.1
  64.9 50.1 %collective-permute-start.2 = (bf16[64,320]{1,0:T(8,128)(2,1)}, bf16[64,320]{1,0:T(8,128)(2,1)S(1)}, u32[]{:S(2)}, u32[]{:S(2)}) collective-permute-start(bf16[64,320]{1,0:T(8,128)(2,1)} %get-tuple-element.667), channel_id=1, source_target_pairs={{0,8},{8,16},{16,24},{24,0},{1,9},{9,17},{17,25},{25,1},{2,10},{10... | collective-permute-start | bytes 122888 | tf_op jit(solution)/shard_map/ppermute | solution.py:126
  115.0 1.7 slice.124
  116.7 1.5 slice.125
  118.2 53.6 %collective-permute-done.2 = bf16[64,320]{1,0:T(8,128)(2,1)S(1)} collective-permute-done((bf16[64,320]{1,0:T(8,128)(2,1)}, bf16[64,320]{1,0:T(8,128)(2,1)S(1)}, u32[]{:S(2)}, u32[]{:S(2)}) %collective-permute-start.2) | collective-permute-done | bytes 40992 | tf_op jit(solution)/shard_map/ppermute | solution.py:126
  171.8 53.4 %conditional.7 = (f32[64,10,64]{2,0,1:T(8,128)}, f32[64,128]{1,0:T(8,128)}, f32[64,10]{0,1:T(8,128)}, bf16[1,64,320]{2,1,0:T(8,128)(2,1)}, bf16[64,1,10,64]{3,0,...) conditional(s32[]{:T(128)} %convert_element_type.356, (f32[64,10,64]{2,0,1:T(8,128)}, f32[64,128]{1,0:T(8,128)}, ...), branch_computations={%region_27.28_spmd, %region_28.36_spmd} | conditional | flops 736944576 | bytes 55699912 | solution.py:116
  171.8 0.8 broadcast_in_dim.94
  172.6 3.7 %all-to-all-start = ((bf16[8,64,320]{2,1,0:T(8,128)(2,1)}), bf16[8,64,320]{2,1,0:T(8,128)(2,1)S(1)}, u32[]{:S(2)}, u32[]{:S(2)}) async-start(bf16[8,64,320]{2,1,0:T(8,128)(2,1)} %broadcast_in_dim.94), calls=%async_computation | async-start | bytes 786432 | tf_op jit(solution)/shard_map/cond/branch_1_fun/all_to_all | solution.py:12
  176.3 0.7 reduce.17
  177.2 2.3 copy.329
  179.5 0.7 copy.332
  180.2 0.7 exponential_bitcast_fusion.3
  180.9 1.3 copy_bitcast_fusion.22
  182.2 1.9 all-to-all-done
  184.1 0.2 fusion.89
  184.5 0.2 copy.189
  184.7 0.3 convert_element_type.333
  185.0 2.4 fusion.86
  187.4 0.8 copy.193
  188.2 0.3 multiply_reduce_fusion.18
  188.5 0.7 multiply_reduce_fusion.19
  189.3 0.5 copy.190
  189.8 0.2 reshape.281
  190.0 4.2 %fusion.94 = f32[64,10,128]{2,0,1:T(8,128)S(1)} fusion(bf16[10,2560,128]{2,1,0:T(8,128)(2,1)} %get-tuple-element.243, f32[64,2560]{1,0:T(8,128)S(1)} %reshape.281, f32[2560]{0:T(1024)S(1)} %reduce.17, f32[64]{0:T(128)S(1)} %add_rsqrt_fusion.3), kind=kOutput, calls=%fused_computation.192 | convolution fusion | flops 419921920 | bytes 7547136 | tf_op jit(solution)/shard_map/cond/branch_1_fun/sd,hdc->shc/dot_general | solution.py:56
  194.5 8.5 %multiply_reduce_fusion.15 = f32[64,10,64]{2,1,0:T(8,128)S(1)} fusion(bf16[64,10,64,128]{3,2,1,0:T(8,128)(2,1)} %get-tuple-element.251, f32[64,128]{1,0:T(8,128)S(1)} %get-tuple-element.611), kind=kLoop, calls=%fused_computation.171 | loop fusion | flops 15687680 | bytes 10682368 | tf_op jit(solution)/shard_map/cond/branch_1_fun/reduce_sum | solution.py:76
  203.1 0.8 multiply_exponential_fusion.3
  203.9 0.4 multiply_reduce_fusion.16
  204.4 1.9 multiply_convert_fusion.7
  206.6 1.7 copy.195
  208.3 2.3 convolution_convert_fusion.3
  210.6 1.3 reshape.277
  212.1 11.4 %all_to_all.32 = bf16[8,64,322]{2,1,0:T(8,128)(2,1)S(1)} all-to-all(bf16[8,64,322]{2,1,0:T(8,128)(2,1)S(1)} %pad_maximum_fusion.6), channel_id=1, replica_groups=mesh['section'=4,'tensor'=8] {'tensor'}, dimensions={0} | all-to-all | bytes 659456 | tf_op jit(solution)/shard_map/cond/branch_1_fun/all_to_all | solution.py:98
  223.5 0.2 fusion.109
  223.7 1.5 fusion.105
  225.2 1.2 copy.220
  226.4 0.8 copy.219
  227.2 1.9 maximum_bitcast_fusion
  229.0 1.5 maximum_bitcast_fusion.1
  230.6 10.4 %add_convert_fusion = bf16[1,64,10,64,128]{4,3,2,1,0:T(8,128)(2,1)} fusion(bf16[1,64,10,64,128]{4,3,2,1,0:T(8,128)(2,1)} %param.41, f32[64,128]{1,0:T(8,128)} %get-tuple-element.286, f32[64,10,64]{2,1,0:T(8,128)S(1)} %copy.220, f32[64,10]{1,0:T(8,128)S(1)} %copy.219), kind=kLoop, calls=%fused_computation.231 | loop fusion | flops 26214400 | bytes 21170688 | tf_op jit(solution)/shard_map/convert_element_type | solution.py:138
  (48 shorter events, 1.3 us)
Async XLA Ops:
  3.9 57.3 %collective-permute-start = (bf16[64,320]{1,0:T(8,128)(2,1)}, bf16[64,320]{1,0:T(8,128)(2,1)S(1)}, u32[]{:S(2)}, u32[]{:S(2)}) collective-permute-start(bf16[64,320]{1,0:T(8,128)(2,1)} %get-tuple-element.273), channel_id=1, source_target_pairs={{0,8},{8,16},{16,24},{24,0},{1,9},{9,17},{17,25},{25,1},{2,10},{10... | collective-permute-start | bytes 122888 | tf_op jit(solution)/shard_map/ppermute | solution.py:126
  61.2 3.7 %collective-permute-start.1 = (bf16[64,320]{1,0:T(8,128)(2,1)}, bf16[64,320]{1,0:T(8,128)(2,1)S(1)}, u32[]{:S(2)}, u32[]{:S(2)}) collective-permute-start(bf16[64,320]{1,0:T(8,128)(2,1)} %get-tuple-element.274), channel_id=1, source_target_pairs={{0,8},{8,16},{16,24},{24,0},{1,9},{9,17},{17,25},{25,1},{2,10},{10... | collective-permute-start | bytes 122888 | tf_op jit(solution)/shard_map/ppermute | solution.py:126
  64.9 106.9 %copy-start.11 = (bf16[1,64,3,256]{3,1,2,0:T(8,128)(2,1)S(1)}, bf16[1,64,3,256]{3,1,2,0:T(8,128)(2,1)}, u32[]{:S(2)}) copy-start(bf16[1,64,3,256]{3,1,2,0:T(8,128)(2,1)} %param.40) | copy-start | bytes 294916
  64.9 106.9 %collective-permute-start.2 = (bf16[64,320]{1,0:T(8,128)(2,1)}, bf16[64,320]{1,0:T(8,128)(2,1)S(1)}, u32[]{:S(2)}, u32[]{:S(2)}) collective-permute-start(bf16[64,320]{1,0:T(8,128)(2,1)} %get-tuple-element.667), channel_id=1, source_target_pairs={{0,8},{8,16},{16,24},{24,0},{1,9},{9,17},{17,25},{25,1},{2,10},{10... | collective-permute-start | bytes 122888 | tf_op jit(solution)/shard_map/ppermute | solution.py:126
  171.8 0.8 copy-start.24
  171.8 16.4 %copy-start.28 = (f32[1,4,256]{2,1,0:T(4,128)S(1)}, f32[1,4,256]{2,1,0:T(4,128)}, u32[]{:S(2)}) copy-start(f32[1,4,256]{2,1,0:T(4,128)} %get-tuple-element.248) | copy-start | bytes 12292 | tf_op jit(solution)/shard_map/cond
  171.8 16.7 %copy-start.33 = (f32[1,256]{1,0:T(1,128)S(1)}, f32[1,256]{1,0:T(1,128)}, u32[]{:S(2)}) copy-start(f32[1,256]{1,0:T(1,128)} %get-tuple-element.249) | copy-start | bytes 3076 | tf_op jit(solution)/shard_map/cond
  172.6 11.5 %all-to-all-start = ((bf16[8,64,320]{2,1,0:T(8,128)(2,1)}), bf16[8,64,320]{2,1,0:T(8,128)(2,1)S(1)}, u32[]{:S(2)}, u32[]{:S(2)}) async-start(bf16[8,64,320]{2,1,0:T(8,128)(2,1)} %broadcast_in_dim.94), calls=%async_computation | async-start | bytes 786432 | tf_op jit(solution)/shard_map/cond/branch_1_fun/all_to_all | solution.py:12
  185.0 4.4 %copy-start.18 = (bf16[64,2560]{1,0:T(8,128)(2,1)}, bf16[64,2560]{1,0:T(8,128)(2,1)S(1)}, u32[]{:S(2)}) copy-start(bf16[64,2560]{1,0:T(8,128)(2,1)S(1)} %convert_element_type.333) | copy-start | bytes 983044 | tf_op jit(solution)/shard_map/cond
  194.2 8.9 %copy-start.19 = (bf16[64,2560]{1,0:T(8,128)(2,1)S(1)}, bf16[64,2560]{1,0:T(8,128)(2,1)}, u32[]{:S(2)}) copy-start(bf16[64,2560]{1,0:T(8,128)(2,1)} %copy-done.18) | copy-start | bytes 983044 | tf_op jit(solution)/shard_map/cond
  194.2 8.9 %copy-start.41 = (bf16[1,2560,10]{1,2,0:T(8,128)(2,1)S(1)}, bf16[1,2560,10]{1,2,0:T(8,128)(2,1)}, u32[]{:S(2)}) copy-start(bf16[1,2560,10]{1,2,0:T(8,128)(2,1)} %get-tuple-element.240) | copy-start | bytes 153604 | tf_op jit(solution)/shard_map/cond
  194.2 8.9 %copy-start.45 = (f32[1,10]{1,0:T(1,128)S(1)}, f32[1,10]{1,0:T(1,128)}, u32[]{:S(2)}) copy-start(f32[1,10]{1,0:T(1,128)} %get-tuple-element.241) | copy-start | bytes 124 | tf_op jit(solution)/shard_map/cond
  194.2 9.7 %copy-start.6 = (bf16[1,64,3,10,64]{4,3,2,1,0:T(8,128)(2,1)S(1)}, bf16[1,64,3,10,64]{4,3,2,1,0:T(8,128)(2,1)}, u32[]{:S(2)}) copy-start(bf16[1,64,3,10,64]{4,3,2,1,0:T(8,128)(2,1)} %copy.329) | copy-start | bytes 737284 | tf_op jit(solution)/shard_map/cond
  194.3 10.0 %copy-start.12 = (bf16[64,1,10,64]{3,0,2,1:T(8,128)(2,1)}, bf16[64,1,10,64]{3,0,2,1:T(8,128)(2,1)S(1)}, u32[]{:S(2)}) copy-start(bf16[64,1,10,64]{3,0,2,1:T(8,128)(2,1)S(1)} %fusion.101) | copy-start | bytes 245764 | tf_op jit(solution)/shard_map/cond
  194.5 9.9 %copy-start.29 = (f32[10,64]{1,0:T(8,128)S(1)}, f32[10,64]{1,0:T(8,128)}, u32[]{:S(2)}) copy-start(f32[10,64]{1,0:T(8,128)} %get-tuple-element.615) | copy-start | bytes 7684 | tf_op jit(solution)/shard_map/cond
  194.5 9.9 %copy-start.37 = (f32[1,10]{1,0:T(1,128)S(1)}, f32[1,10]{1,0:T(1,128)}, u32[]{:S(2)}) copy-start(f32[1,10]{1,0:T(1,128)} %get-tuple-element.252) | copy-start | bytes 124 | tf_op jit(solution)/shard_map/cond
  194.5 13.8 %copy-start.3 = (bf16[1,10,64,2560]{3,2,1,0:T(8,128)(2,1)S(1)}, bf16[1,10,64,2560]{3,2,1,0:T(8,128)(2,1)}, u32[]{:S(2)}) copy-start(bf16[1,10,64,2560]{3,2,1,0:T(8,128)(2,1)} %get-tuple-element.254) | copy-start | bytes 9830404 | tf_op jit(solution)/shard_map/cond
  204.4 20.9 %copy-start.13 = (bf16[64,1,10,64]{3,0,2,1:T(8,128)(2,1)S(1)}, bf16[64,1,10,64]{3,0,2,1:T(8,128)(2,1)}, u32[]{:S(2)}) copy-start(bf16[64,1,10,64]{3,0,2,1:T(8,128)(2,1)} %copy-done.12) | copy-start | bytes 245764 | tf_op jit(solution)/shard_map/cond

commit v2 on v1

v2 whole, which is shorter than its diff:
```python
import functools

import jax
import jax.numpy as jnp
from jax import lax
from jax.experimental import pallas as pl
from jax.experimental.pallas import tpu as pltpu
from jax.sharding import PartitionSpec as P

epsilon = 1e-05
row_block = 8
wide_lanes = 128
input_count = 16
in_flight = 3


def silu(value):
    return value / (1.0 + jnp.exp(-value))


def split_two(value):
    high = value.astype(jnp.bfloat16)
    low = (value - high.astype(jnp.float32)).astype(jnp.bfloat16)
    return high, low


def layer_math(
    shares,
    gain,
    w_heads,
    w_bc,
    w_dt,
    dt_bias,
    a_log,
    d_skip,
    conv_x_weight,
    conv_x_bias,
    conv_bc_weight,
    conv_bc_bias,
    inner_gain,
    w_out,
    conv_x_state,
    conv_bc_state,
    state,
    wait_heads,
    wait_out,
    wait_state,
    sent,
    conv_x_out,
    conv_bc_out,
    stepped_out,
    decay_out,
    b_out,
    old_part,
    gated_buf,
):
    parts, streams, share_cols = shares.shape
    heads, width, lanes = w_heads.shape
    head_size = lanes // 2
    state_size = w_bc.shape[1] // 2
    inner = heads * head_size
    blocks = streams // row_block

    wide = [shares[at].astype(jnp.float32) for at in range(parts)]
    square = sum(jnp.sum(piece * piece, axis=-1, keepdims=True) for piece in wide)
    scale = lax.rsqrt(square / width + epsilon)
    normed = jnp.concatenate(wide, axis=1) * scale * gain[...]
    normed = normed.astype(jnp.bfloat16)

    bc_fresh = jnp.dot(normed, w_bc[...], preferred_element_type=jnp.float32).astype(jnp.bfloat16)
    taps = conv_bc_weight[...]
    count = taps.shape[0]
    for tap in range(count - 2):
        conv_bc_out[tap] = conv_bc_state[tap + 1]
        conv_x_out[tap] = conv_x_state[tap + 1]
    conv_bc_out[count - 2] = bc_fresh
    bc_sum = bc_fresh.astype(jnp.float32) * taps[count - 1 : count]
    for tap in range(count - 1):
        bc_sum = bc_sum + conv_bc_state[tap].astype(jnp.float32) * taps[tap : tap + 1]
    bc_conv = silu(bc_sum + conv_bc_bias[...])
    b_input = bc_conv[:, :state_size]
    c_output = bc_conv[:, state_size:]
    b_out[...] = b_input
    overlap = jnp.sum(b_input * c_output, axis=-1, keepdims=True)
    dt_raw = lax.dot_general(
        normed, w_dt[...], (((1,), (1,)), ((), ())), preferred_element_type=jnp.float32
    )
    step_size = jax.nn.softplus(dt_raw + dt_bias[...])
    decay = jnp.exp(-step_size * jnp.exp(a_log[...]))
    decay_out[...] = decay

    c_high, c_low = split_two(c_output)
    row_at = lax.broadcasted_iota(jnp.int32, (row_block, inner), 0)
    for block in range(blocks):
        wait_state(block)
        first = block * row_block
        both = jnp.concatenate(
            [
                c_high[first : first + row_block].astype(jnp.float32),
                c_low[first : first + row_block].astype(jnp.float32),
            ],
            axis=0,
        ).astype(jnp.bfloat16)
        kept = jnp.zeros((row_block, inner), jnp.float32)
        for row in range(row_block):
            product = lax.dot_general(
                both,
                state[first + row],
                (((1,), (1,)), ((), ())),
                preferred_element_type=jnp.float32,
            )
            kept = jnp.where(row_at == row, product[:row_block] + product[row_block:], kept)
        old_part[first : first + row_block, :] = kept

    squares = jnp.zeros((streams, 1), jnp.float32)
    for head in range(heads):
        wait_heads(head)
        zx = jnp.dot(normed, w_heads[head], preferred_element_type=jnp.float32)
        gate = zx[:, :head_size]
        x_fresh = zx[:, head_size:].astype(jnp.bfloat16)
        conv_x_out[count - 2, head] = x_fresh
        taps = conv_x_weight[head]
        x_sum = x_fresh.astype(jnp.float32) * taps[count - 1 : count]
        for tap in range(count - 1):
            x_sum = x_sum + conv_x_state[tap, head].astype(jnp.float32) * taps[tap : tap + 1]
        x_conv = silu(x_sum + conv_x_bias[head])
        stepped = x_conv * step_size[:, head : head + 1]
        span = slice(head * head_size, (head + 1) * head_size)
        stepped_out[:, span] = stepped
        faded = decay[:, head : head + 1]
        y_out = faded * old_part[:, span] + stepped * overlap + d_skip[:, head : head + 1] * x_conv
        gated = y_out * silu(gate)
        squares = squares + jnp.sum(gated * gated, axis=-1, keepdims=True)
        gated_buf[:, span] = gated * inner_gain[head]

    scaled = gated_buf[...].astype(jnp.bfloat16)
    wait_out()
    partial = jnp.dot(scaled, w_out[...], preferred_element_type=jnp.float32)
    tail_cols = sent.shape[2] - share_cols
    high, low = split_two(squares)
    lane_at = lax.broadcasted_iota(jnp.int32, (streams, tail_cols), 1)
    tail = jnp.where(
        lane_at == 0,
        high.astype(jnp.float32),
        jnp.where(lane_at == 1, low.astype(jnp.float32), 0.0),
    )
    for at in range(parts):
        piece = partial[:, at * share_cols : (at + 1) * share_cols]
        sent[at] = jnp.concatenate([piece, tail], axis=1).astype(jnp.bfloat16)


def layer_body(shares, *refs):
    inputs = refs[:input_count]
    outputs = refs[input_count : input_count + 6]
    buffers = refs[input_count + 6 : 2 * input_count + 6]
    small_sem, heads_sem, out_sem, state_sem, old_part, gated_buf = refs[2 * input_count + 6 :]
    heads = inputs[1].shape[0]
    blocks = inputs[-1].shape[0] // row_block
    large = (1, 12, input_count - 1)

    def rows(block):
        return pl.ds(block * row_block, row_block)

    small_copies = [
        pltpu.make_async_copy(inputs[at], buffers[at], small_sem.at[at])
        for at in range(input_count)
        if at not in large
    ]
    state_copies = [
        pltpu.make_async_copy(inputs[-1].at[rows(at)], buffers[-1].at[rows(at)], state_sem.at[at])
        for at in range(blocks)
    ]
    head_copies = [
        pltpu.make_async_copy(inputs[1].at[at], buffers[1].at[at], heads_sem.at[at])
        for at in range(heads)
    ]
    out_copy = pltpu.make_async_copy(inputs[12], buffers[12], out_sem)
    for copy in small_copies:
        copy.start()
    ordered = state_copies + head_copies + [out_copy]
    for copy in ordered[:in_flight]:
        copy.start()
    for copy in small_copies:
        copy.wait()

    def arrive(at):
        ordered[at].wait()
        if at + in_flight < len(ordered):
            ordered[at + in_flight].start()

    layer_math(
        shares,
        *buffers,
        lambda head: arrive(blocks + head),
        lambda: arrive(blocks + heads),
        arrive,
        *outputs,
        old_part,
        gated_buf,
    )


def update_body(old, stepped, decay, b_input, out, state, fresh_buf, in_sems, sems):
    streams, inner, size = state.shape
    heads = decay.shape[1]
    head_size = inner // heads
    blocks = streams // row_block

    def enter(block):
        rows = pl.ds(block * row_block, row_block)
        return pltpu.make_async_copy(old.at[rows], state.at[rows], in_sems.at[block])

    def leave(block):
        rows = pl.ds(block * row_block, row_block)
        return pltpu.make_async_copy(fresh_buf.at[rows], out.at[rows], sems.at[block])

    def step(block, carry):
        first = pl.multiple_of(block * row_block, row_block)
        enter(block).wait()

        @pl.when(block + in_flight < blocks)
        def _():
            enter(block + in_flight).start()

        stepped_t = jnp.transpose(stepped[pl.ds(first, row_block), :])
        faded_rows = decay[pl.ds(first, row_block), :]
        b_rows = b_input[pl.ds(first, row_block), :]
        for row in range(row_block):
            b_row = jnp.broadcast_to(b_rows[row : row + 1], (head_size, size))
            for head in range(heads):
                span = slice(head * head_size, (head + 1) * head_size)
                column = jnp.broadcast_to(stepped_t[span, row : row + 1], (head_size, size))
                faded = jnp.broadcast_to(faded_rows[row : row + 1, head : head + 1], (head_size, size))
                fresh = faded * state[first + row, span].astype(jnp.float32) + column * b_row
                fresh_buf[first + row, span] = fresh.astype(jnp.bfloat16)
        leave(block).start()
        return carry

    for block in range(min(in_flight, blocks)):
        enter(block).start()
    lax.fori_loop(0, blocks, step, 0)
    for block in range(blocks):
        leave(block).wait()


def whole(memory=pltpu.VMEM):
    return pl.BlockSpec(memory_space=memory)


def run_layer(*operands):
    shares, gain, w_heads, w_bc, w_dt = operands[:5]
    w_out, conv_x_state, conv_bc_state, state = operands[13:]
    parts, streams, share_cols = shares.shape
    heads, width, lanes = w_heads.shape
    head_size = lanes // 2
    inner = heads * head_size
    both = w_bc.shape[1]
    sent_cols = -(-(share_cols + 2) // wide_lanes) * wide_lanes
    flops = 2 * streams * (width * (heads * lanes + both + inner)) + 2 * state.size
    moved = 2 * (w_heads.size + w_bc.size + w_out.size + state.size)
    return pl.pallas_call(
        layer_body,
        in_specs=[whole()] + [whole(pltpu.HBM) for _ in operands[1:]],
        out_specs=tuple(whole() for _ in range(6)),
        out_shape=(
            jax.ShapeDtypeStruct((parts, streams, sent_cols), jnp.bfloat16),
            jax.ShapeDtypeStruct(conv_x_state.shape, jnp.bfloat16),
            jax.ShapeDtypeStruct(conv_bc_state.shape, jnp.bfloat16),
            jax.ShapeDtypeStruct((streams, inner), jnp.float32),
            jax.ShapeDtypeStruct((streams, heads), jnp.float32),
            jax.ShapeDtypeStruct((streams, both // 2), jnp.float32),
        ),
        scratch_shapes=[pltpu.VMEM(operand.shape, operand.dtype) for operand in operands[1:]]
        + [
            pltpu.SemaphoreType.DMA((input_count,)),
            pltpu.SemaphoreType.DMA((heads,)),
            pltpu.SemaphoreType.DMA(()),
            pltpu.SemaphoreType.DMA((streams // row_block,)),
            pltpu.VMEM((streams, inner), jnp.float32),
            pltpu.VMEM((streams, inner), jnp.float32),
        ],
        compiler_params=pltpu.CompilerParams(vmem_limit_bytes=44 * 1024 * 1024),
        cost_estimate=pl.CostEstimate(flops=flops, transcendentals=0, bytes_accessed=moved),
        name="layer",
    )(*operands)


def run_update(state, stepped, decay, b_input):
    blocks = state.shape[0] // row_block
    return pl.pallas_call(
        update_body,
        in_specs=[whole(pltpu.HBM)] + [whole() for _ in range(3)],
        out_specs=whole(pltpu.HBM),
        out_shape=jax.ShapeDtypeStruct(state.shape, state.dtype),
        scratch_shapes=[
            pltpu.VMEM(state.shape, state.dtype),
            pltpu.VMEM(state.shape, state.dtype),
            pltpu.SemaphoreType.DMA((blocks,)),
            pltpu.SemaphoreType.DMA((blocks,)),
        ],
        compiler_params=pltpu.CompilerParams(vmem_limit_bytes=24 * 1024 * 1024),
        cost_estimate=pl.CostEstimate(
            flops=40 * state.size, transcendentals=0, bytes_accessed=4 * state.size
        ),
        name="update",
    )(state, stepped, decay, b_input)


def gather_shares(share):
    count = lax.axis_size("tensor")
    spread = jnp.broadcast_to(share[None], (count,) + share.shape)
    return lax.all_to_all(spread, "tensor", 0, 0, tiled=True)


def shards(
    hidden_in,
    pre_gain,
    w_zx,
    w_bc,
    w_dt,
    dt_bias,
    a_log,
    d_skip,
    conv_x_weight,
    conv_x_bias,
    conv_bc_weight,
    conv_bc_bias,
    inner_gain,
    w_out,
    conv_x_state,
    conv_bc_state,
    ssm_state,
):
    section_count = lax.axis_size("section")
    tensor_count = lax.axis_size("tensor")
    section_at = lax.axis_index("section")
    streams, share_cols = hidden_in.shape
    width = w_zx.shape[1]
    heads = w_zx.shape[2]
    head_size = w_zx.shape[3] // 2
    both = w_bc.shape[2]
    inner = heads * head_size
    all_channels = inner * tensor_count
    state = ssm_state[0].reshape(streams, inner, both // 2)
    x_old = jnp.transpose(conv_x_state[0], (1, 2, 0, 3))
    bc_old = jnp.transpose(conv_bc_state[0], (1, 0, 2))
    layer_args = (
        pre_gain,
        jnp.transpose(w_zx[0], (1, 0, 2)),
        w_bc[0],
        jnp.transpose(w_dt[0]),
        dt_bias,
        a_log,
        d_skip,
        jnp.transpose(conv_x_weight[0], (1, 0, 2)),
        jnp.transpose(conv_x_bias, (1, 0, 2)),
        conv_bc_weight[0],
        conv_bc_bias,
        jnp.transpose(inner_gain, (1, 0, 2)),
        w_out[0].reshape(inner, width),
        x_old,
        bc_old,
        state,
    )

    def live(share, with_update):
        shares = gather_shares(share)
        sent, x_new, bc_new, stepped, decay, b_input = run_layer(shares, *layer_args)
        got = lax.all_to_all(sent, "tensor", 0, 0, tiled=True)
        factors = (stepped, decay, b_input)
        if with_update:
            factors = run_update(state, *factors)
        total = jnp.sum(got.astype(jnp.float32), axis=0)
        squares = total[:, share_cols : share_cols + 1] + total[:, share_cols + 1 : share_cols + 2]
        factor = lax.rsqrt(squares / all_channels + epsilon)
        fresh = (share.astype(jnp.float32) + total[:, :share_cols] * factor).astype(jnp.bfloat16)
        return fresh, x_new, bc_new, factors

    def rest(share, old, with_update):
        if with_update:
            return old[:3] + (run_update(state, *old[3]),)
        return old

    incoming = hidden_in
    kept = (
        jnp.zeros_like(hidden_in),
        x_old,
        bc_old,
        (
            jnp.zeros((streams, inner), jnp.float32),
            jnp.zeros((streams, heads), jnp.float32),
            jnp.zeros((streams, both // 2), jnp.float32),
        ),
    )
    for tick in range(section_count):
        last = tick + 1 == section_count
        kept = lax.cond(
            section_at == tick,
            lambda share, old, last=last: live(share, last),
            lambda share, old, last=last: rest(share, old, last),
            incoming,
            kept,
        )
        if not last:
            ring = [(at, (at + 1) % section_count) for at in range(section_count)]
            incoming = lax.ppermute(kept[0], "section", ring)
    section_share, x_new, bc_new, state_new = kept
    return (
        section_share[None],
        jnp.transpose(x_new, (2, 0, 1, 3))[None],
        jnp.transpose(bc_new, (1, 0, 2))[None],
        state_new.reshape(ssm_state.shape),
    )


def solution(mesh):
    placed = (
        P(None, "tensor"),
        P("section", None),
        P("section", None, "tensor", None),
        P("section", None, None),
        P("section", None, "tensor"),
        P("section", "tensor"),
        P("section", "tensor"),
        P("section", "tensor"),
        P("section", None, "tensor", None),
        P("section", "tensor", None),
        P("section", None, None),
        P("section", None),
        P("section", "tensor", None),
        P("section", "tensor", None, None),
        P("section", None, None, "tensor", None),
        P("section", None, None, None),
        P("section", None, "tensor", None, None),
    )
    return jax.shard_map(
        shards,
        mesh=mesh,
        in_specs=placed,
        out_specs=(
            P("section", None, "tensor"),
            P("section", None, None, "tensor", None),
            P("section", None, None, None),
            P("section", None, "tensor", None, None),
        ),
        check_vma=False,
    )
```

time: 242 us -> 165 us (0.68)
  starting transfers between devices: 112 us -> 79.2 us
  other arithmetic: 28.8 us -> 0.33 us
  Pallas kernels: 0 us -> 26.1 us
  waiting for transfers between devices: 58.5 us -> 42.8 us
  local copies, waits for them, and re-layouts: 19.7 us -> 4.06 us
  matrix products: 9.73 us -> 0 us
    ppermute x3, starting transfers between devices: 108 us -> 75.8 us  [shards(): incoming = lax.ppermute(kept[0], 'section', ring)]
    pallas_call x0 -> x2, Pallas kernels: none -> 26.1 us  [the longest x1 14.5 us: run_layer(): pl.pallas_call(layer_body, in_specs=[whole()] + [whole(pltpu.HBM) for _ i...]
    ppermute x3, waiting for transfers between devices: 56.6 us -> 42.8 us  [shards(): incoming = lax.ppermute(kept[0], 'section', ring)]
    convert_element_type x5 -> x1, other arithmetic: 12.3 us -> 0.09 us  [live(): (share.astype(jnp.float32) + total[:, :share_cols] * factor).astype(jnp.b...]
    reduce_sum x7 -> x1, other arithmetic: 10.4 us -> 0.05 us  [live(): total = jnp.sum(got.astype(jnp.float32), axis=0)]
    dot_general x4 -> x0, matrix products: 9.73 us -> none  [the longest x1 4.16 us: live(): jnp.einsum('sd,hdc->shc', normed, w_heads, preferred_element_type=jnp.flo...]
    broadcast_in_dim x3 -> x0, other arithmetic: 4.87 us -> none  [the longest x1 1.85 us: shards(): conv_x_new[None]]
    broadcast_in_dim x9 -> x3, local copies, waits for them, and re-layouts: 3.67 us -> 0.02 us  [the longest x1 0.01 us: shards(): jnp.zeros((streams, inner), jnp.float32)]
  transfers between devices with their start and end apart: 4 -> 4, of which waited for: 4 -> 3; matrix products, arithmetic and copies ran while one was open for 4% -> 0% of each run, Pallas kernels for 0% -> 7%
where the time goes in v2:
time: 165 us; the launch traced here: 164 us
  starting transfers between devices  79.2 us (48%)
  waiting for transfers between devices  42.8 us (26%)
  Pallas kernels  26.1 us (16%)
  blocking collectives  10.9 us (7%)
  local copies, waits for them, and re-layouts  4.06 us (2%)
    ppermute x3, starting transfers between devices, shards(): incoming = lax.ppermute(kept[0], 'section', ring)  75.8 us
    ppermute x3, waiting for transfers between devices, shards(): incoming = lax.ppermute(kept[0], 'section', ring)  42.8 us
    pallas_call x1, Pallas kernels, run_layer(): pl.pallas_call(layer_body, in_specs=[whole()] + [whole(pltpu.HBM) for _ i...  14.5 us
    pallas_call x1, Pallas kernels, run_update(): pl.pallas_call(update_body, in_specs=[whole(pltpu.HBM)] + [whole() for _...  11.7 us
    all_to_all x1, blocking collectives, gather_shares(): return lax.all_to_all(spread, 'tensor', 0, 0, tiled=True)  10.9 us
    all_to_all x1, starting transfers between devices, live(): got = lax.all_to_all(sent, 'tensor', 0, 0, tiled=True)  3.46 us
    cond x2, local copies, waits for them, and re-layouts  3.38 us
  transfers between devices with their start and end apart: 4, of which 3 were waited for; matrix products, arithmetic and copies ran while one was open for 0% of the time, Pallas kernels for 7%

profile of v2, /device:TPU:3, one launch (start us, length us, event | category | flops | bytes accessed | tf_op | source)
XLA Modules:
  0.0 164.5 jit_solution(12061638287875089849)
XLA Ops:
  0.6 3.4 %conditional.4 = (bf16[64,320]{1,0:T(8,128)(2,1)S(1)}, bf16[3,10,64,64]{3,2,1,0:T(8,128)(2,1)}, bf16[3,64,256]{2,1,0:T(8,128)(2,1)}, f32[64,640]{1,0:T(8,128)S(1...) conditional(s32[]{:T(128)} %convert_element_type.51, (bf16[3,10,64,64]{3,2,1,0:T(8,128)(2,1)}, ...), branch_computations={%region_0.0_spmd, %region_1.0_spmd} | conditional | flops 723968192 | bytes 24257612 | solution.py:397
  0.6 1.5 copy.29
  2.2 1.8 %copy.28 = bf16[3,10,64,64]{3,2,1,0:T(8,128)(2,1)} copy(bf16[3,10,64,64]{3,2,1,0:T(8,128)(2,1)} %get-tuple-element.326) | data formatting | bytes 491520 | tf_op jit(solution)/shard_map/cond
  4.1 39.8 %collective-permute-start = (bf16[64,320]{1,0:T(8,128)(2,1)S(1)}, bf16[64,320]{1,0:T(8,128)(2,1)S(1)}, u32[]{:S(2)}, u32[]{:S(2)}) collective-permute-start(bf16[64,320]{1,0:T(8,128)(2,1)S(1)} %get-tuple-element.296), channel_id=1, source_target_pairs={{0,8},{8,16},{16,24},{24,0},{1,9},{9,17},{17,25},{25,1},{2,10},{10... | collective-permute-start | bytes 122888 | tf_op jit(solution)/shard_map/ppermute | solution.py:406
  43.9 1.2 collective-permute-done
  45.1 2.3 %collective-permute-start.1 = (bf16[64,320]{1,0:T(8,128)(2,1)S(1)}, bf16[64,320]{1,0:T(8,128)(2,1)S(1)}, u32[]{:S(2)}, u32[]{:S(2)}) collective-permute-start(bf16[64,320]{1,0:T(8,128)(2,1)S(1)} %get-tuple-element.297), channel_id=1, source_target_pairs={{0,8},{8,16},{16,24},{24,0},{1,9},{9,17},{17,25},{25,1},{2,10},{10... | collective-permute-start | bytes 122888 | tf_op jit(solution)/shard_map/ppermute | solution.py:406
  47.4 1.2 collective-permute-done.1
  48.6 33.6 %collective-permute-start.2 = (bf16[64,320]{1,0:T(8,128)(2,1)S(1)}, bf16[64,320]{1,0:T(8,128)(2,1)S(1)}, u32[]{:S(2)}, u32[]{:S(2)}) collective-permute-start(bf16[64,320]{1,0:T(8,128)(2,1)S(1)} %get-tuple-element.301), channel_id=1, source_target_pairs={{0,8},{8,16},{16,24},{24,0},{1,9},{9,17},{17,25},{25,1},{2,10},{10... | collective-permute-start | bytes 122888 | tf_op jit(solution)/shard_map/ppermute | solution.py:406
  82.2 40.5 %collective-permute-done.2 = bf16[64,320]{1,0:T(8,128)(2,1)S(1)} collective-permute-done((bf16[64,320]{1,0:T(8,128)(2,1)S(1)}, bf16[64,320]{1,0:T(8,128)(2,1)S(1)}, u32[]{:S(2)}, u32[]{:S(2)}) %collective-permute-start.2) | collective-permute-done | bytes 40992 | tf_op jit(solution)/shard_map/ppermute | solution.py:406
  122.6 41.2 %conditional.7 = (bf16[64,320]{1,0:T(8,128)(2,1)S(1)}, bf16[3,10,64,64]{3,2,1,0:T(8,128)(2,1)}, bf16[3,64,256]{2,1,0:T(8,128)(2,1)}, bf16[1,64,10,64,128]{4,3,2,1,0:T(8,128)(2,1)}) conditional(s32[]{:T(128)} %convert_element_type.48, (bf16[64,640,128]{2,1,0:T(8,128)(2,1)}, f32[64,640]{1,0:T(8,128)S(1)}, f32[64,10]{1,0:T(8,128)S(1)}, ...), branch_computations={%region_9.0_spmd, %region_10.0_spmd} | conditional | flops 933683392 | bytes 45458496 | solution.py:397
  122.7 10.9 %all_to_all.38.shares = bf16[8,64,320]{2,1,0:T(8,128)(2,1)S(1)} all-to-all(bf16[8,64,320]{2,1,0:T(8,128)(2,1)S(1)} %broadcast_in_dim.34), channel_id=1, replica_groups=mesh['section'=4,'tensor'=8] {'tensor'}, dimensions={0} | all-to-all | bytes 655360 | tf_op jit(solution)/shard_map/cond/branch_1_fun/all_to_all | solution.py:312
  133.6 14.5 %layer.7 = (bf16[8,64,384]{2,1,0:T(8,128)(2,1)}, bf16[3,10,64,64]{3,2,1,0:T(8,128)(2,1)}, bf16[3,64,256]{2,1,0:T(8,128)(2,1)}, f32[64,640]{1,0:T(8,128)S(1)}, f3...) custom-call(bf16[8,64,320]{2,1,0:T(8,128)(2,1)S(1)} %all_to_all.38.shares, f32[1,2560]{1,0:T(1,128)} %get-tuple-element.258.refs_0_, ...), custom_call_target="tpu_custom_call" | custom-call | flops 723517440 | bytes 21626880 | tf_op jit(solution)/shard_map/cond/branch_1_fun/layer/pallas_call | solution.py:261
  148.0 3.5 %all-to-all-start.7 = ((bf16[8,64,384]{2,1,0:T(8,128)(2,1)}), bf16[8,64,384]{2,1,0:T(8,128)(2,1)S(1)}, u32[]{:S(2)}, u32[]{:S(2)}) async-start(bf16[8,64,384]{2,1,0:T(8,128)(2,1)} %get-tuple-element.274), calls=%async_computation.7 | async-start | bytes 786432 | tf_op jit(solution)/shard_map/cond/branch_1_fun/all_to_all | solution.py:369
  151.5 11.7 %update.3 = bf16[64,640,128]{2,1,0:T(8,128)(2,1)} custom-call(bf16[64,640,128]{2,1,0:T(8,128)(2,1)} %get-tuple-element.273.refs_15_.old, f32[64,640]{1,0:T(8,128)S(1)} %get-tuple-element.277.stepped, f32[64,10]{1,0:T(8,128)S(1)} %get-tuple-element.278.decay, f32[64,128]{1,0:T(8,128)S(1)} %get-tuple-element.279.b_input), custom_call_target="tpu_custom_call" | custom-call | flops 209715200 | bytes 20971520 | tf_op jit(solution)/shard_map/cond/branch_1_fun/update/pallas_call | solution.py:290
  163.2 0.0 all-to-all-done.7
  163.2 0.1 convert_reduce_fusion.3
  163.2 0.2 fusion.23
  163.4 0.1 fusion.19
  163.8 0.0 copy-start.1
  163.8 0.6 copy-done.1
  (7 shorter events, 0.1 us)
Async XLA Ops:
  4.1 41.0 %collective-permute-start = (bf16[64,320]{1,0:T(8,128)(2,1)S(1)}, bf16[64,320]{1,0:T(8,128)(2,1)S(1)}, u32[]{:S(2)}, u32[]{:S(2)}) collective-permute-start(bf16[64,320]{1,0:T(8,128)(2,1)S(1)} %get-tuple-element.296), channel_id=1, source_target_pairs={{0,8},{8,16},{16,24},{24,0},{1,9},{9,17},{17,25},{25,1},{2,10},{10... | collective-permute-start | bytes 122888 | tf_op jit(solution)/shard_map/ppermute | solution.py:406
  45.1 3.5 %collective-permute-start.1 = (bf16[64,320]{1,0:T(8,128)(2,1)S(1)}, bf16[64,320]{1,0:T(8,128)(2,1)S(1)}, u32[]{:S(2)}, u32[]{:S(2)}) collective-permute-start(bf16[64,320]{1,0:T(8,128)(2,1)S(1)} %get-tuple-element.297), channel_id=1, source_target_pairs={{0,8},{8,16},{16,24},{24,0},{1,9},{9,17},{17,25},{25,1},{2,10},{10... | collective-permute-start | bytes 122888 | tf_op jit(solution)/shard_map/ppermute | solution.py:406
  48.6 74.1 %collective-permute-start.2 = (bf16[64,320]{1,0:T(8,128)(2,1)S(1)}, bf16[64,320]{1,0:T(8,128)(2,1)S(1)}, u32[]{:S(2)}, u32[]{:S(2)}) collective-permute-start(bf16[64,320]{1,0:T(8,128)(2,1)S(1)} %get-tuple-element.301), channel_id=1, source_target_pairs={{0,8},{8,16},{16,24},{24,0},{1,9},{9,17},{17,25},{25,1},{2,10},{10... | collective-permute-start | bytes 122888 | tf_op jit(solution)/shard_map/ppermute | solution.py:406
  148.0 15.1 %all-to-all-start.7 = ((bf16[8,64,384]{2,1,0:T(8,128)(2,1)}), bf16[8,64,384]{2,1,0:T(8,128)(2,1)S(1)}, u32[]{:S(2)}, u32[]{:S(2)}) async-start(bf16[8,64,384]{2,1,0:T(8,128)(2,1)} %get-tuple-element.274), calls=%async_computation.7 | async-start | bytes 786432 | tf_op jit(solution)/shard_map/cond/branch_1_fun/all_to_all | solution.py:369
  163.8 0.6 copy-start.1
